TPU v7x, 32 devices: a whole 2x2x4 slice. The times are simulated.
32 devices in a mesh: space: 16 (over z, y, core), probe: 2 (over x).
Axes of the slice: x: 2, y: 2, z: 4, core: 2. Of those that a mesh axis runs over, the one named last changes fastest.
Arguments:
- positions: bfloat16 [128, 3, 32], P('space'), may hold values from -4.3125 to 4.3125
- probes: bfloat16 [128, 512, 128], P('space', 'probe'), may hold values from -4 to 4
- neighbours: int32 [128, 15], P('space'), may hold values from -1 to 127, as said below
Outputs:
- density: bfloat16 [128, 128, 15, 128], P('probe', 'space')
- forces: float32 [128, 3, 32], P('space')
Inputs may be any that keep to these rules, and one draw needn't show every extreme that they name: `neighbours`: slot 0 of each cluster names the cluster itself. Clusters are held 8 to an index of space in order; every other entry is -1 or a cluster held by the same index of space or by the index one before or one after it, cyclically. The clusters named in one row are distinct.
All inputs are finite; a program needn't handle non-finite values.
Results may differ from a plain program's by a relative error of at most 0.0018.
The roundings to bfloat16 on the way count: a program that leaves them out, or rounds other values in their place, can miss the bound.
Values may be sent and summed in bfloat16 or wider, within the bound.
A program may use at most 64 MiB of HBM per device.

v0:
```python
import functools

import jax
import jax.numpy as jnp
from jax import lax
from jax.experimental import pallas as pl
from jax.experimental.pallas import tpu as pltpu
from jax.sharding import PartitionSpec as P

SS_SIGMA = -1.938
SP_SIGMA = 1.745
PP_SIGMA = 3.05
PP_PI = -1.075
PP_DIFF = PP_SIGMA - PP_PI
BOND_LENGTH = 2.35
SOFT_SQUARE = 0.25
CELL_EDGE = 10.86
COEFF_ZERO = 0.6
COEFF_ONE = -0.7
COEFF_TWO = 0.45
MESH = pl.DeviceIdType.MESH
LANES = 128
F32 = jnp.float32
BF16 = jnp.bfloat16


def offsets():
    half = CELL_EDGE / 2.0
    table = [(0.0, 0.0, 0.0)]
    for x in (-1.0, 1.0):
        for y in (-1.0, 1.0):
            for z in (-1.0, 1.0):
                table.append((x * half, y * half, z * half))
    for axis in range(3):
        for sign in (1.0, -1.0):
            entry = [0.0, 0.0, 0.0]
            entry[axis] = sign * CELL_EDGE
            table.append(tuple(entry))
    return table


SHIFTS = offsets()


def kernel(
    sizes,
    names_ref,
    wanted_ref,
    positions_ref,
    probes_ref,
    dens_ref,
    force_ref,
    slot_ref,
    alive_ref,
    posc_ref,
    near,
    rest,
    near_pos,
    ham,
    scaled,
    pair,
    maxima,
    first,
    one_t,
    mix,
    row_mix,
    dense,
    stage,
    col_force,
    pull,
    own_pull,
    arrived,
    local_sem,
    pos_s,
    pos_r,
    probe_s,
    probe_r,
    own_s,
    own_r,
    fwd_s,
    fwd_r,
    chip_s,
    chip_r,
    max_s,
    max_r,
    one_s,
    one_r,
    mix_s,
    mix_r,
    pull_s,
    pull_r,
):
    space, wide, count, atoms, slots, span, share = sizes
    orbitals = 4 * atoms
    total = span * wide
    s = lax.axis_index("space")
    q = lax.axis_index("probe")
    up = lax.rem(s + 1, space)
    down = lax.rem(s + space - 1, space)
    before, own, after = pl.ds(0, count), pl.ds(count, count), pl.ds(2 * count, count)
    core = lax.rem(s, 2)
    mate = s + 1 - 2 * core
    far_side = pl.ds(core * (2 * count), count)

    def send(src, dst, ss, rs, to_space, to_probe):
        return pltpu.make_async_remote_copy(
            src_ref=src,
            dst_ref=dst,
            send_sem=ss,
            recv_sem=rs,
            device_id={"space": to_space, "probe": to_probe},
            device_id_type=MESH,
        )

    load = pltpu.make_async_copy(probes_ref, near.at[own], local_sem)
    load.start()

    barrier = pltpu.get_barrier_semaphore()

    def greet(d, carry):
        pl.semaphore_signal(
            barrier,
            inc=1,
            device_id={"space": lax.rem(s + d, space), "probe": q},
            device_id_type=MESH,
        )
        return carry

    lax.fori_loop(1, space, greet, 0)
    for e in range(1, wide):
        for to in (s, up, down):
            pl.semaphore_signal(
                barrier,
                inc=1,
                device_id={"space": to, "probe": lax.rem(q + e, wide)},
                device_id_type=MESH,
            )

    def fold(x):
        return (
            x
            + pltpu.roll(x, atoms, 1)
            + pltpu.roll(x, 2 * atoms, 1)
            + pltpu.roll(x, 3 * atoms, 1)
        )

    near_pos[:, own, :atoms] = positions_ref[...].astype(F32)
    narrow = lax.broadcasted_iota(jnp.int32, (count, orbitals), 1) < atoms
    for m in range(3):
        wide_row = fold(jnp.where(narrow, near_pos[m, own], 0.0))
        near_pos[m, own] = wide_row
        tall = jnp.transpose(wide_row)
        for c in range(count):
            posc_ref[c, m] = jnp.broadcast_to(tall[:atoms, c : c + 1], (atoms, orbitals))

    def find_slots(c, carry):
        for k in range(slots):
            name = names_ref[c, k]
            held = jnp.maximum(name, 0)
            place = lax.rem(lax.div(held, count) - s + 1 + space, space) * count
            place = place + lax.rem(held, count)
            slot_ref[c, k] = jnp.where(name >= 0, jnp.minimum(place, 3 * count - 1), count)
            alive_ref[c, k] = jnp.where(name >= 0, 1.0, 0.0)
        return carry

    lax.fori_loop(0, count, find_slots, 0)
    pl.semaphore_wait(barrier, space - 1 + 3 * (wide - 1))

    pos_up = send(near_pos.at[:, own], near_pos.at[:, before], pos_s.at[0], pos_r.at[0], up, q)
    pos_down = send(near_pos.at[:, own], near_pos.at[:, after], pos_s.at[1], pos_r.at[1], down, q)
    pos_up.start()
    pos_down.start()
    load.wait()
    probe_up = send(
        near.at[own], near.at[before], probe_s.at[0], probe_r.at[0], up, q
    )
    probe_down = send(
        near.at[own], near.at[after], probe_s.at[1], probe_r.at[1], down, q
    )
    probe_up.start()
    probe_down.start()
    own_out = []
    for e in range(1, wide):
        copy = send(
            near.at[own],
            rest.at[e - 1, own],
            own_s.at[e - 1],
            own_r.at[e - 1],
            s,
            lax.rem(q + e, wide),
        )
        copy.start()
        own_out.append(copy)
    pos_up.wait_recv()
    pos_down.wait_recv()

    lane = lax.broadcasted_iota(jnp.int32, (atoms, orbitals), 1)
    group = lane // atoms
    is_s = group == 0
    is_p = [group == 1, group == 2, group == 3]
    pp = [jnp.where(m, PP_PI, 0.0).astype(F32) for m in is_p]

    def build(c, peak):
        rows = [posc_ref[c, m] for m in range(3)]
        sums = [jnp.zeros((atoms, orbitals), F32) for _ in range(4)]
        for k in range(slots):
            place = slot_ref[c, k]
            alive = alive_ref[c, k]
            d = [
                (near_pos[m, pl.ds(place, 1), :] + SHIFTS[k][m]) - rows[m] for m in range(3)
            ]
            square = d[0] * d[0] + d[1] * d[1] + d[2] * d[2] + SOFT_SQUARE
            inv = lax.rsqrt(square)
            l = [x * inv for x in d]
            g = jnp.exp(1.0 - square * (1.0 / (BOND_LENGTH * BOND_LENGTH))) * alive
            beta = jnp.where(
                is_s, 0.0, jnp.where(is_p[0], l[0], jnp.where(is_p[1], l[1], l[2]))
            )
            coef_s = jnp.where(is_s, SS_SIGMA, SP_SIGMA * beta)
            coef_p = jnp.where(is_s, -SP_SIGMA, PP_DIFF * beta)
            parts = [coef_s * g] + [(l[m] * coef_p + pp[m]) * g for m in range(3)]
            for a in range(4):
                ham[c, a * atoms : (a + 1) * atoms, k * orbitals : (k + 1) * orbitals] = parts[a]
                sums[a] = sums[a] + jnp.abs(parts[a])
            pair[c, k, 0] = jnp.zeros_like(g)
            for m in range(3):
                pair[c, k, 1 + m] = l[m]
            pair[c, k, 4] = beta
            pair[c, k, 5] = g * inv
            pair[c, k, 6] = g * (square * inv) * (2.0 / (BOND_LENGTH * BOND_LENGTH))
        for a in range(4):
            peak = jnp.maximum(peak, jnp.sum(sums[a], axis=1, keepdims=True))
        return peak

    peak = lax.fori_loop(0, count, build, jnp.zeros((atoms, 1), F32))
    top = jnp.max(peak, axis=0, keepdims=True)
    maxima[s] = jnp.broadcast_to(top, (8, LANES))

    def max_copy(d):
        return send(
            maxima.at[s],
            maxima.at[s],
            max_s.at[d],
            max_r.at[d],
            lax.rem(s + d, space),
            q,
        )

    def start_max(d, carry):
        max_copy(d).start()
        return carry

    def wait_max(d, carry):
        max_copy(d).wait()
        return carry

    lax.fori_loop(1, space, start_max, 0)
    lax.fori_loop(1, space, wait_max, 0)
    spectral = jnp.max(maxima[...], axis=0)[0:1]
    shrink = 1.0 / spectral

    probe_up.wait_recv()
    probe_down.wait_recv()
    fwd_out = []
    for e in range(1, wide):
        copy = send(
            near.at[far_side],
            rest.at[e - 1, far_side],
            fwd_s.at[e - 1],
            fwd_r.at[e - 1],
            s,
            lax.rem(q + e, wide),
        )
        copy.start()
        fwd_out.append(copy)

    def one_copies(c):
        return (
            send(one_t.at[count + c], one_t.at[c], one_s.at[0, c], one_r.at[0, c], up, q),
            send(
                one_t.at[count + c], one_t.at[2 * count + c], one_s.at[1, c], one_r.at[1, c], down, q
            ),
        )

    def term_one(c, carry):
        for k in range(slots):
            part = pl.ds(k * orbitals, orbitals)
            scaled[c, :, part] = (ham[c, :, part] * shrink).astype(BF16)
        right = jnp.concatenate([near[slot_ref[c, k]] for k in range(slots)], axis=1)
        term = lax.dot_general(
            scaled[c], right, (((1,), (1,)), ((), ())), preferred_element_type=F32
        )
        first[c] = term
        one_t[count + c] = term.astype(BF16)
        for copy in one_copies(c):
            copy.start()
        return carry

    lax.fori_loop(0, count, term_one, 0)

    chip_out = []
    for e in range(1, wide):
        own_out[e - 1].wait_recv()
        copy = send(
            rest.at[e - 1, own],
            rest.at[e - 1, far_side],
            chip_s.at[e - 1],
            chip_r.at[e - 1],
            mate,
            q,
        )
        copy.start()
        chip_out.append(copy)

    def wait_one(c, carry):
        for copy in one_copies(c):
            copy.wait()
        return carry

    lax.fori_loop(0, count, wait_one, 0)

    eye = (
        lax.broadcasted_iota(jnp.int32, (orbitals, orbitals), 0)
        == lax.broadcasted_iota(jnp.int32, (orbitals, orbitals), 1)
    ).astype(BF16)
    my_rows = pl.ds(pl.multiple_of(q * share, share), share)

    def mix_copies(c):
        copies = []
        for e in range(1, wide):
            to = lax.rem(q + e, wide)
            copies.append(
                send(
                    mix.at[c, pl.ds(pl.multiple_of(to * share, share), share)],
                    row_mix.at[q, c],
                    mix_s.at[e - 1, c],
                    mix_r.at[e - 1, c],
                    s,
                    to,
                )
            )
        return copies

    def term_two(c, carry):
        right = jnp.concatenate([one_t[slot_ref[c, k]] for k in range(slots)], axis=0)
        term = jnp.dot(scaled[c], right, preferred_element_type=F32)
        probe = lax.dot_general(
            eye, near[count + c], (((1,), (1,)), ((), ())), preferred_element_type=F32
        )
        second = 2.0 * term - probe
        mix[c] = (COEFF_ZERO * probe + COEFF_ONE * first[c] + COEFF_TWO * second).astype(BF16)
        row_mix[q, c] = mix[c, my_rows, :]
        for copy in mix_copies(c):
            copy.start()
        return carry

    lax.fori_loop(0, count, term_two, 0)

    def product(w, t):
        left = row_mix[lax.rem(q + wide - w, wide)].reshape(count * share, span)
        source = near if w == 0 else rest.at[w - 1]
        right = jnp.concatenate([source[2 * t], source[2 * t + 1]], axis=1)
        part = jnp.dot(left, right, preferred_element_type=F32)
        return [
            part[:, h * orbitals : (h + 1) * orbitals].reshape(count, share, orbitals)
            for h in range(2)
        ]

    def overlap_own(t, carry):
        dense[2 * t], dense[2 * t + 1] = product(0, t)
        return carry

    lax.fori_loop(0, 3 * count // 2, overlap_own, 0)

    for copy in fwd_out + chip_out:
        copy.wait_recv()

    def wait_mix(c, carry):
        for copy in mix_copies(c):
            copy.wait()
        return carry

    lax.fori_loop(0, count, wait_mix, 0)

    def overlap_rest(t, carry):
        for w in range(1, wide):
            low, high = product(w, t)
            dense[2 * t] = dense[2 * t] + low
            dense[2 * t + 1] = dense[2 * t + 1] + high
        return carry

    lax.fori_loop(0, 3 * count // 2, overlap_rest, 0)

    height = min(atoms, share)
    turns = share // height
    start_atom = lax.rem(q * share, atoms)
    rows = pl.ds(pl.multiple_of(start_atom, height), height)
    s_mask = jnp.where(is_s[:height], 1.0, 0.0).astype(F32)
    p_mask = [jnp.where(m[:height], 1.0, 0.0).astype(F32) for m in is_p]
    row_iota = lax.broadcasted_iota(jnp.int32, (height, orbitals), 0) + start_atom
    hit = jnp.where(row_iota == lax.rem(lane[:height], atoms), 1.0, 0.0).astype(F32)
    scale = 1.0 / float(total) ** 0.5

    def eight(x):
        return jnp.sum(x.reshape(height // 8, 8, orbitals), axis=0)

    def forces(c, carry):
        row_total = [jnp.zeros((8, orbitals), F32) for _ in range(3)]
        for t in range(turns):
            kind = (q * share) // atoms + t
            ws = jnp.where(kind == 0, 1.0, 0.0).astype(F32)
            wr = [jnp.where(kind == m + 1, 1.0, 0.0).astype(F32) for m in range(3)]
            wv = PP_PI * (wr[0] * p_mask[0] + wr[1] * p_mask[1] + wr[2] * p_mask[2])
            wv = wv + (ws * SS_SIGMA) * s_mask
            acc = [jnp.zeros((height, orbitals), F32) for _ in range(5)]
            for k in range(slots):
                sample = dense[slot_ref[c, k], c, pl.ds(t * height, height), :] * alive_ref[c, k]
                alpha = pair[c, k, kind, rows, :]
                beta = pair[c, k, 4, rows, :]
                c_one = PP_DIFF * alpha + ws * SP_SIGMA
                c_two = PP_DIFF * beta - SP_SIGMA * s_mask
                cross = alpha * c_two
                bracket = (ws * SP_SIGMA) * beta + cross + wv
                lean = sample * pair[c, k, 5, rows, :]
                x = lean * c_one
                y = lean * c_two
                drag = lean * (c_one * beta + cross) + sample * pair[c, k, 6, rows, :] * bracket
                z = [drag * pair[c, k, 1 + m, rows, :] for m in range(3)]
                group_of = [x, y] + z
                for i in range(5):
                    acc[i] = acc[i] + group_of[i]
                sx, sy, z0, z1, z2 = [eight(v) for v in group_of]
                for m, zm in enumerate((z0, z1, z2)):
                    value = sx * p_mask[m][:8] + sy * wr[m] - zm
                    if t > 0:
                        value = value + col_force[k, m]
                    col_force[k, m] = value
            for m in range(3):
                value = acc[0] * p_mask[m] + acc[1] * wr[m] - acc[2 + m]
                value = jnp.sum(value, axis=1, keepdims=True) * hit
                row_total[m] = row_total[m] + eight(value)
        column = jnp.concatenate(
            [jnp.sum(col_force[:, m], axis=1) for m in range(3)], axis=1
        )
        picked = jnp.where(wanted_ref[pl.ds(c, 1), :] == held_ids, 1.0, 0.0)
        moved = jnp.dot(
            picked, column, precision=lax.Precision.HIGHEST, preferred_element_type=F32
        )
        for m in range(3):
            pull[m] = pull[m] + moved[:, m * orbitals : (m + 1) * orbitals]
            line = jnp.sum(row_total[m], axis=0, keepdims=True)
            own_pull[m, pl.ds(c, 1), :] = line
        return carry

    ids = lax.broadcasted_iota(jnp.int32, (3 * count, slots), 0)
    held_ids = jnp.where(
        ids < count,
        ids + down * count,
        jnp.where(ids < 2 * count, ids - count + s * count, ids - 2 * count + up * count),
    )
    for m in range(3):
        pull[m] = jnp.zeros((3 * count, orbitals), F32)

    def density(k, carry):
        for c in range(count):
            sample = dense[slot_ref[c, k], c] * (alive_ref[c, k] * scale)
            stage[pl.ds(c, share, stride=count), :] = sample
        dens_ref[:, k] = stage[...].reshape(share, count, orbitals).astype(dens_ref.dtype)
        return carry

    lax.fori_loop(0, slots, density, 0)
    lax.fori_loop(0, count, forces, 0)

    for m in range(3):
        pull[m] = fold(pull[m])
        pull[m, own] = pull[m, own] - own_pull[m]
    arrived[1, q] = pull[:, own]
    pull_out = []
    for e in range(wide):
        to = lax.rem(q + e, wide)
        moves = [(pull.at[:, after], 0, up), (pull.at[:, before], 2, down)]
        if e > 0:
            moves.append((pull.at[:, own], 1, s))
        for src, kind, to_space in moves:
            copy = send(
                src, arrived.at[kind, q], pull_s.at[kind, e], pull_r.at[kind, e], to_space, to
            )
            copy.start()
            pull_out.append(copy)
    for copy in pull_out:
        copy.wait()
    result = None
    for kind in range(3):
        for w in range(wide):
            part = arrived[kind, w]
            result = part if result is None else result + part
    force_ref[...] = (result * (-1.0 / total))[:, :, :atoms]

    for copy in [pos_up, pos_down, probe_up, probe_down] + own_out + fwd_out + chip_out:
        copy.wait_send()


def per_device(positions, probes, neighbours):
    count, _, atoms = positions.shape
    slots = neighbours.shape[1]
    orbitals = 4 * atoms
    span = probes.shape[1]
    space = lax.axis_size("space")
    wide = lax.axis_size("probe")
    share = orbitals // wide
    sizes = (space, wide, count, atoms, slots, span, share)
    smem = pl.BlockSpec(memory_space=pltpu.SMEM)
    vmem = pl.BlockSpec(memory_space=pltpu.VMEM)
    dma = pltpu.SemaphoreType.DMA
    peers = max(wide - 1, 1)
    density, force = pl.pallas_call(
        functools.partial(kernel, sizes),
        name="band_forces",
        out_shape=(
            jax.ShapeDtypeStruct((share, slots, count, orbitals), BF16),
            jax.ShapeDtypeStruct((3, count, atoms), F32),
        ),
        in_specs=[smem, vmem, vmem, pl.BlockSpec(memory_space=pl.ANY)],
        out_specs=(vmem, vmem),
        scratch_shapes=[
            pltpu.SMEM((count, slots), jnp.int32),
            pltpu.SMEM((count, slots), F32),
            pltpu.VMEM((count, 3, atoms, orbitals), F32),
            pltpu.VMEM((3 * count, span, orbitals), BF16),
            pltpu.VMEM((peers, 3 * count, span, orbitals), BF16),
            pltpu.VMEM((3, 3 * count, orbitals), F32),
            pltpu.VMEM((count, orbitals, slots * orbitals), F32),
            pltpu.VMEM((count, orbitals, slots * orbitals), BF16),
            pltpu.VMEM((count, slots, 7, atoms, orbitals), F32),
            pltpu.VMEM((space, 8, LANES), F32),
            pltpu.VMEM((count, orbitals, span), F32),
            pltpu.VMEM((3 * count, orbitals, span), BF16),
            pltpu.VMEM((count, orbitals, span), BF16),
            pltpu.VMEM((wide, count, share, span), BF16),
            pltpu.VMEM((3 * count, count, share, orbitals), F32),
            pltpu.VMEM((share * count, orbitals), F32),
            pltpu.VMEM((slots, 3, 8, orbitals), F32),
            pltpu.VMEM((3, 3 * count, orbitals), F32),
            pltpu.VMEM((3, count, orbitals), F32),
            pltpu.VMEM((3, wide, 3, count, orbitals), F32),
            dma,
            dma((2,)),
            dma((2,)),
            dma((2,)),
            dma((2,)),
            dma((peers,)),
            dma((peers,)),
            dma((peers,)),
            dma((peers,)),
            dma((peers,)),
            dma((peers,)),
            dma((space,)),
            dma((space,)),
            dma((2, count)),
            dma((2, count)),
            dma((peers, count)),
            dma((peers, count)),
            dma((3, wide)),
            dma((3, wide)),
        ],
        compiler_params=pltpu.CompilerParams(
            collective_id=0, has_side_effects=True, vmem_limit_bytes=60 * 1024 * 1024
        ),
    )(neighbours, neighbours, jnp.transpose(positions, (1, 0, 2)), probes)
    return jnp.transpose(density, (0, 2, 1, 3)), jnp.transpose(force, (1, 0, 2))


def solution(mesh):
    in_specs = (P("space", None, None), P("space", "probe", None), P("space", None))
    out_specs = (P("probe", "space", None, None), P("space", None, None))
    return jax.shard_map(
        per_device, mesh=mesh, in_specs=in_specs, out_specs=out_specs, check_vma=False
    )
```

profile of v0, /device:TPU:0, one launch (start us, length us, event | category | flops | bytes accessed | tf_op | source)
XLA Modules:
  0.0 61.1 jit_solution(10253182383860362478)
XLA Ops:
  0.6 56.9 %band_forces.1 = (bf16[64,15,8,128]{3,2,1,0:T(8,128)(2,1)}, f32[3,8,32]{2,1,0:T(8,128)}) custom-call(s32[8,15]{1,0:T(8,128)} %wanted_ref.1, s32[8,15]{1,0:T(8,128)} %wanted_ref.1, bf16[3,8,32]{2,1,0:T(8,128)(2,1)} %bitcast.5, bf16[8,256,128]{2,1,0:T(8,128)(2,1)} %probes_ref.1), custom_call_target="tpu_custom_call" | custom-call | tf_op jit(solution)/shard_map/band_forces/pallas_call | solution.py:516
  57.5 0.0 copy-start
  57.5 3.0 %copy.7 = bf16[64,8,15,128]{3,1,2,0:T(8,128)(2,1)} copy(bf16[64,8,15,128]{3,1,2,0:T(8,128)(2,1)} %bitcast.3) | data formatting | bytes 3932160
  60.5 0.0 copy-done
  60.5 0.6 copy.8
Async XLA Ops:
  57.5 3.0 %copy-start = (f32[3,8,32]{2,1,0:T(8,128)S(1)}, f32[3,8,32]{2,1,0:T(8,128)}, u32[]{:S(2)}) copy-start(f32[3,8,32]{2,1,0:T(8,128)} %get-tuple-element.5) | copy-start | bytes 9220
where the time goes:
time: 61.3 us; the launch traced here: 61.1 us
  Pallas kernels  56.9 us (93%)
  local copies, waits for them, and re-layouts  3.57 us (6%)
  between operations  0.65 us (1%)
    pallas_call x1, Pallas kernels, per_device(): pl.pallas_call(functools.partial(kernel, sizes), name='band_forces', out_...  56.9 us
    unnamed x4, local copies, waits for them, and re-layouts  3.57 us

commit v1 on v0

--- a/solution.py
+++ b/solution.py
@@ -44,14 +44,16 @@
 
 def kernel(
     sizes,
-    names_ref,
-    wanted_ref,
+    neighbours_ref,
     positions_ref,
     probes_ref,
     dens_ref,
     force_ref,
+    names_ref,
     slot_ref,
     alive_ref,
+    wanted_ref,
+    raw_pos,
     posc_ref,
     near,
     rest,
@@ -59,7 +61,9 @@
     ham,
     scaled,
     pair,
-    maxima,
+    top_out,
+    top_in,
+    slope,
     first,
     one_t,
     mix,
@@ -67,8 +71,8 @@
     dense,
     stage,
     col_force,
+    row_force,
     pull,
-    own_pull,
     arrived,
     local_sem,
     pos_s,
@@ -112,29 +116,63 @@
             device_id_type=MESH,
         )
 
-    load = pltpu.make_async_copy(probes_ref, near.at[own], local_sem)
-    load.start()
+    steps = space.bit_length() - 1
+    partners = []
+    for j in range(steps):
+        bit = lax.rem(lax.div(s, 2**j), 2)
+        partners.append(s + 2**j * (1 - 2 * bit))
 
     barrier = pltpu.get_barrier_semaphore()
 
-    def greet(d, carry):
+    def greet(to_space, to_probe):
         pl.semaphore_signal(
             barrier,
             inc=1,
-            device_id={"space": lax.rem(s + d, space), "probe": q},
+            device_id={"space": to_space, "probe": to_probe},
             device_id_type=MESH,
         )
-        return carry
-
-    lax.fori_loop(1, space, greet, 0)
+
+    for to in partners + [up, down]:
+        greet(to, q)
     for e in range(1, wide):
         for to in (s, up, down):
-            pl.semaphore_signal(
-                barrier,
-                inc=1,
-                device_id={"space": to, "probe": lax.rem(q + e, wide)},
-                device_id_type=MESH,
-            )
+            greet(to, lax.rem(q + e, wide))
+
+    loads = [
+        pltpu.make_async_copy(src, dst, local_sem.at[i])
+        for i, (src, dst) in enumerate(
+            [
+                (positions_ref, raw_pos.at[1]),
+                (neighbours_ref, names_ref),
+                (neighbours_ref, wanted_ref),
+                (probes_ref, near.at[own]),
+            ]
+        )
+    ]
+    for load in loads:
+        load.start()
+    pl.semaphore_wait(barrier, steps + 2 + 3 * (wide - 1))
+
+    pos_up = send(positions_ref, raw_pos.at[0], pos_s.at[0], pos_r.at[0], up, q)
+    pos_down = send(positions_ref, raw_pos.at[2], pos_s.at[1], pos_r.at[1], down, q)
+    pos_up.start()
+    pos_down.start()
+    probe_up = send(probes_ref, near.at[before], probe_s.at[0], probe_r.at[0], up, q)
+    probe_down = send(probes_ref, near.at[after], probe_s.at[1], probe_r.at[1], down, q)
+    probe_up.start()
+    probe_down.start()
+    own_out = []
+    for e in range(1, wide):
+        copy = send(
+            probes_ref,
+            rest.at[e - 1, own],
+            own_s.at[e - 1],
+            own_r.at[e - 1],
+            s,
+            lax.rem(q + e, wide),
+        )
+        copy.start()
+        own_out.append(copy)
 
     def fold(x):
         return (
@@ -144,12 +182,18 @@
             + pltpu.roll(x, 3 * atoms, 1)
         )
 
-    near_pos[:, own, :atoms] = positions_ref[...].astype(F32)
+    def spread(part):
+        rows = pl.ds(part * count, count)
+        for m in range(3):
+            near_pos[m, rows, :atoms] = raw_pos[part, m].astype(F32)
+            near_pos[m, rows] = fold(jnp.where(narrow, near_pos[m, rows], 0.0))
+
+    for load in loads[:3]:
+        load.wait()
     narrow = lax.broadcasted_iota(jnp.int32, (count, orbitals), 1) < atoms
+    spread(1)
     for m in range(3):
-        wide_row = fold(jnp.where(narrow, near_pos[m, own], 0.0))
-        near_pos[m, own] = wide_row
-        tall = jnp.transpose(wide_row)
+        tall = jnp.transpose(near_pos[m, own])
         for c in range(count):
             posc_ref[c, m] = jnp.broadcast_to(tall[:atoms, c : c + 1], (atoms, orbitals))
 
@@ -164,35 +208,10 @@
         return carry
 
     lax.fori_loop(0, count, find_slots, 0)
-    pl.semaphore_wait(barrier, space - 1 + 3 * (wide - 1))
-
-    pos_up = send(near_pos.at[:, own], near_pos.at[:, before], pos_s.at[0], pos_r.at[0], up, q)
-    pos_down = send(near_pos.at[:, own], near_pos.at[:, after], pos_s.at[1], pos_r.at[1], down, q)
-    pos_up.start()
-    pos_down.start()
-    load.wait()
-    probe_up = send(
-        near.at[own], near.at[before], probe_s.at[0], probe_r.at[0], up, q
-    )
-    probe_down = send(
-        near.at[own], near.at[after], probe_s.at[1], probe_r.at[1], down, q
-    )
-    probe_up.start()
-    probe_down.start()
-    own_out = []
-    for e in range(1, wide):
-        copy = send(
-            near.at[own],
-            rest.at[e - 1, own],
-            own_s.at[e - 1],
-            own_r.at[e - 1],
-            s,
-            lax.rem(q + e, wide),
-        )
-        copy.start()
-        own_out.append(copy)
     pos_up.wait_recv()
+    spread(0)
     pos_down.wait_recv()
+    spread(2)
 
     lane = lax.broadcasted_iota(jnp.int32, (atoms, orbitals), 1)
     group = lane // atoms
@@ -200,9 +219,38 @@
     is_p = [group == 1, group == 2, group == 3]
     pp = [jnp.where(m, PP_PI, 0.0).astype(F32) for m in is_p]
 
-    def build(c, peak):
+    def peak_of(c, peak):
         rows = [posc_ref[c, m] for m in range(3)]
         sums = [jnp.zeros((atoms, orbitals), F32) for _ in range(4)]
+        for k in range(0, slots, 4):
+            picked = range(k, min(k + 4, slots))
+            alive = jnp.zeros((1, orbitals), F32)
+            column = [jnp.zeros((1, orbitals), F32) for _ in range(3)]
+            for i, t in enumerate(picked):
+                here = group[:1] == i
+                alive = jnp.where(here, alive_ref[c, t], alive)
+                place = slot_ref[c, t]
+                for m in range(3):
+                    column[m] = jnp.where(
+                        here, near_pos[m, pl.ds(place, 1), :] + SHIFTS[t][m], column[m]
+                    )
+            d = [column[m] - rows[m] for m in range(3)]
+            square = d[0] * d[0] + d[1] * d[1] + d[2] * d[2] + SOFT_SQUARE
+            inv = lax.rsqrt(square)
+            u = [jnp.abs(x) * inv for x in d]
+            g = jnp.exp(1.0 - square * (1.0 / (BOND_LENGTH * BOND_LENGTH))) * alive
+            sums[0] = sums[0] + g * ((u[0] + u[1] + u[2]) * SP_SIGMA - SS_SIGMA)
+            for a in range(3):
+                others = u[(a + 1) % 3] + u[(a + 2) % 3]
+                value = u[a] * (others * PP_DIFF + SP_SIGMA)
+                value = value + jnp.abs(u[a] * u[a] * PP_DIFF + PP_PI)
+                sums[1 + a] = sums[1 + a] + g * value
+        for a in range(4):
+            peak = jnp.maximum(peak, jnp.sum(sums[a], axis=1, keepdims=True))
+        return peak
+
+    def build(c, carry):
+        rows = [posc_ref[c, m] for m in range(3)]
         for k in range(slots):
             place = slot_ref[c, k]
             alive = alive_ref[c, k]
@@ -221,44 +269,30 @@
             parts = [coef_s * g] + [(l[m] * coef_p + pp[m]) * g for m in range(3)]
             for a in range(4):
                 ham[c, a * atoms : (a + 1) * atoms, k * orbitals : (k + 1) * orbitals] = parts[a]
-                sums[a] = sums[a] + jnp.abs(parts[a])
             pair[c, k, 0] = jnp.zeros_like(g)
             for m in range(3):
                 pair[c, k, 1 + m] = l[m]
             pair[c, k, 4] = beta
             pair[c, k, 5] = g * inv
             pair[c, k, 6] = g * (square * inv) * (2.0 / (BOND_LENGTH * BOND_LENGTH))
-        for a in range(4):
-            peak = jnp.maximum(peak, jnp.sum(sums[a], axis=1, keepdims=True))
-        return peak
-
-    peak = lax.fori_loop(0, count, build, jnp.zeros((atoms, 1), F32))
-    top = jnp.max(peak, axis=0, keepdims=True)
-    maxima[s] = jnp.broadcast_to(top, (8, LANES))
-
-    def max_copy(d):
-        return send(
-            maxima.at[s],
-            maxima.at[s],
-            max_s.at[d],
-            max_r.at[d],
-            lax.rem(s + d, space),
-            q,
-        )
-
-    def start_max(d, carry):
-        max_copy(d).start()
-        return carry
-
-    def wait_max(d, carry):
-        max_copy(d).wait()
-        return carry
-
-    lax.fori_loop(1, space, start_max, 0)
-    lax.fori_loop(1, space, wait_max, 0)
-    spectral = jnp.max(maxima[...], axis=0)[0:1]
-    shrink = 1.0 / spectral
-
+        return carry
+
+    peak = lax.fori_loop(0, count, peak_of, jnp.zeros((atoms, 1), F32))
+    top = jnp.broadcast_to(jnp.max(peak, axis=0, keepdims=True), (8, LANES))
+    order = [0] + list(range(2, steps)) + ([1] if steps > 1 else [])
+    done = 0
+    for t, j in enumerate(order):
+        top_out[j] = top
+        copy = send(top_out.at[j], top_in.at[j], max_s.at[j], max_r.at[j], partners[j], q)
+        copy.start()
+        until = count if t == len(order) - 1 else count * (t + 1) // len(order)
+        lax.fori_loop(done, until, build, 0)
+        done = until
+        copy.wait()
+        top = jnp.maximum(top, top_in[j])
+    shrink = 1.0 / top[0:1]
+
+    loads[3].wait()
     probe_up.wait_recv()
     probe_down.wait_recv()
     fwd_out = []
@@ -311,6 +345,42 @@
         )
         copy.start()
         chip_out.append(copy)
+
+    height = min(atoms, share)
+    turns = share // height
+    start_atom = lax.rem(q * share, atoms)
+    rows = pl.ds(pl.multiple_of(start_atom, height), height)
+    s_mask = jnp.where(is_s[:height], 1.0, 0.0).astype(F32)
+    p_mask = [jnp.where(m[:height], 1.0, 0.0).astype(F32) for m in is_p]
+    row_iota = lax.broadcasted_iota(jnp.int32, (height, orbitals), 0) + start_atom
+    hit = jnp.where(row_iota == lax.rem(lane[:height], atoms), 1.0, 0.0).astype(F32)
+    scale = 1.0 / float(total) ** 0.5
+
+    def slopes(c, carry):
+        for t in range(turns):
+            kind = (q * share) // atoms + t
+            ws = jnp.where(kind == 0, 1.0, 0.0).astype(F32)
+            wr = [jnp.where(kind == m + 1, 1.0, 0.0).astype(F32) for m in range(3)]
+            wv = PP_PI * (wr[0] * p_mask[0] + wr[1] * p_mask[1] + wr[2] * p_mask[2])
+            wv = wv + (ws * SS_SIGMA) * s_mask
+            for k in range(slots):
+                alpha = pair[c, k, kind, rows, :]
+                beta = pair[c, k, 4, rows, :]
+                lean = pair[c, k, 5, rows, :]
+                c_one = PP_DIFF * alpha + ws * SP_SIGMA
+                c_two = PP_DIFF * beta - SP_SIGMA * s_mask
+                cross = alpha * c_two
+                bracket = (ws * SP_SIGMA) * beta + cross + wv
+                x = lean * c_one
+                y = lean * c_two
+                drag = lean * (c_one * beta + cross) + pair[c, k, 6, rows, :] * bracket
+                for m in range(3):
+                    slope[c, k, m, t * height : (t + 1) * height] = (
+                        x * p_mask[m] + y * wr[m] - drag * pair[c, k, 1 + m, rows, :]
+                    )
+        return carry
+
+    lax.fori_loop(0, count, slopes, 0)
 
     def wait_one(c, carry):
         for copy in one_copies(c):
@@ -391,66 +461,27 @@
 
     lax.fori_loop(0, 3 * count // 2, overlap_rest, 0)
 
-    height = min(atoms, share)
-    turns = share // height
-    start_atom = lax.rem(q * share, atoms)
-    rows = pl.ds(pl.multiple_of(start_atom, height), height)
-    s_mask = jnp.where(is_s[:height], 1.0, 0.0).astype(F32)
-    p_mask = [jnp.where(m[:height], 1.0, 0.0).astype(F32) for m in is_p]
-    row_iota = lax.broadcasted_iota(jnp.int32, (height, orbitals), 0) + start_atom
-    hit = jnp.where(row_iota == lax.rem(lane[:height], atoms), 1.0, 0.0).astype(F32)
-    scale = 1.0 / float(total) ** 0.5
-
-    def eight(x):
-        return jnp.sum(x.reshape(height // 8, 8, orbitals), axis=0)
+    padded = col_force.shape[1]
 
     def forces(c, carry):
-        row_total = [jnp.zeros((8, orbitals), F32) for _ in range(3)]
-        for t in range(turns):
-            kind = (q * share) // atoms + t
-            ws = jnp.where(kind == 0, 1.0, 0.0).astype(F32)
-            wr = [jnp.where(kind == m + 1, 1.0, 0.0).astype(F32) for m in range(3)]
-            wv = PP_PI * (wr[0] * p_mask[0] + wr[1] * p_mask[1] + wr[2] * p_mask[2])
-            wv = wv + (ws * SS_SIGMA) * s_mask
-            acc = [jnp.zeros((height, orbitals), F32) for _ in range(5)]
-            for k in range(slots):
-                sample = dense[slot_ref[c, k], c, pl.ds(t * height, height), :] * alive_ref[c, k]
-                alpha = pair[c, k, kind, rows, :]
-                beta = pair[c, k, 4, rows, :]
-                c_one = PP_DIFF * alpha + ws * SP_SIGMA
-                c_two = PP_DIFF * beta - SP_SIGMA * s_mask
-                cross = alpha * c_two
-                bracket = (ws * SP_SIGMA) * beta + cross + wv
-                lean = sample * pair[c, k, 5, rows, :]
-                x = lean * c_one
-                y = lean * c_two
-                drag = lean * (c_one * beta + cross) + sample * pair[c, k, 6, rows, :] * bracket
-                z = [drag * pair[c, k, 1 + m, rows, :] for m in range(3)]
-                group_of = [x, y] + z
-                for i in range(5):
-                    acc[i] = acc[i] + group_of[i]
-                sx, sy, z0, z1, z2 = [eight(v) for v in group_of]
-                for m, zm in enumerate((z0, z1, z2)):
-                    value = sx * p_mask[m][:8] + sy * wr[m] - zm
-                    if t > 0:
-                        value = value + col_force[k, m]
-                    col_force[k, m] = value
+        acc = [jnp.zeros((share, orbitals), F32) for _ in range(3)]
+        for k in range(slots):
+            sample = dense[slot_ref[c, k], c]
             for m in range(3):
-                value = acc[0] * p_mask[m] + acc[1] * wr[m] - acc[2 + m]
-                value = jnp.sum(value, axis=1, keepdims=True) * hit
-                row_total[m] = row_total[m] + eight(value)
-        column = jnp.concatenate(
-            [jnp.sum(col_force[:, m], axis=1) for m in range(3)], axis=1
-        )
-        picked = jnp.where(wanted_ref[pl.ds(c, 1), :] == held_ids, 1.0, 0.0)
-        moved = jnp.dot(
-            picked, column, precision=lax.Precision.HIGHEST, preferred_element_type=F32
-        )
+                value = sample * slope[c, k, m]
+                acc[m] = acc[m] + value
+                col_force[c, k, m] = jnp.sum(
+                    value.reshape(share // 8, 8, orbitals), axis=0
+                )
         for m in range(3):
-            pull[m] = pull[m] + moved[:, m * orbitals : (m + 1) * orbitals]
-            line = jnp.sum(row_total[m], axis=0, keepdims=True)
-            own_pull[m, pl.ds(c, 1), :] = line
-        return carry
+            row_force[m, c] = jnp.sum(acc[m].reshape(turns, height, orbitals), axis=0)
+        return carry
+
+    for k in range(slots, padded):
+        for c in range(count):
+            for m in range(3):
+                col_force[c, k, m] = jnp.zeros((8, orbitals), F32)
+    lax.fori_loop(0, count, forces, 0)
 
     ids = lax.broadcasted_iota(jnp.int32, (3 * count, slots), 0)
     held_ids = jnp.where(
@@ -458,22 +489,28 @@
         ids + down * count,
         jnp.where(ids < 2 * count, ids - count + s * count, ids - 2 * count + up * count),
     )
+    blank = jnp.zeros((3 * count, padded - slots), F32)
+    picked = jnp.concatenate(
+        [
+            part
+            for c in range(count)
+            for part in (
+                jnp.where(wanted_ref[c : c + 1, :] == held_ids, 1.0, 0.0),
+                blank,
+            )
+        ],
+        axis=1,
+    )
     for m in range(3):
-        pull[m] = jnp.zeros((3 * count, orbitals), F32)
-
-    def density(k, carry):
-        for c in range(count):
-            sample = dense[slot_ref[c, k], c] * (alive_ref[c, k] * scale)
-            stage[pl.ds(c, share, stride=count), :] = sample
-        dens_ref[:, k] = stage[...].reshape(share, count, orbitals).astype(dens_ref.dtype)
-        return carry
-
-    lax.fori_loop(0, slots, density, 0)
-    lax.fori_loop(0, count, forces, 0)
-
-    for m in range(3):
-        pull[m] = fold(pull[m])
-        pull[m, own] = pull[m, own] - own_pull[m]
+        column = jnp.sum(
+            col_force[:, :, m].reshape(count * padded, 8, orbitals), axis=1
+        )
+        moved = jnp.dot(
+            picked, column, precision=lax.Precision.HIGHEST, preferred_element_type=F32
+        )
+        pull[m] = fold(moved)
+        line = jnp.sum(row_force[m], axis=2, keepdims=True) * hit
+        pull[m, own] = pull[m, own] - jnp.sum(line, axis=1)
     arrived[1, q] = pull[:, own]
     pull_out = []
     for e in range(wide):
@@ -487,6 +524,15 @@
             )
             copy.start()
             pull_out.append(copy)
+
+    def density(k, carry):
+        for c in range(count):
+            sample = dense[slot_ref[c, k], c] * (alive_ref[c, k] * scale)
+            stage[pl.ds(c, share, stride=count), :] = sample
+        dens_ref[:, k] = stage[...].reshape(share, count, orbitals).astype(dens_ref.dtype)
+        return carry
+
+    lax.fori_loop(0, slots, density, 0)
     for copy in pull_out:
         copy.wait()
     result = None
@@ -509,10 +555,10 @@
     wide = lax.axis_size("probe")
     share = orbitals // wide
     sizes = (space, wide, count, atoms, slots, span, share)
-    smem = pl.BlockSpec(memory_space=pltpu.SMEM)
     vmem = pl.BlockSpec(memory_space=pltpu.VMEM)
     dma = pltpu.SemaphoreType.DMA
     peers = max(wide - 1, 1)
+    steps = space.bit_length() - 1
     density, force = pl.pallas_call(
         functools.partial(kernel, sizes),
         name="band_forces",
@@ -520,11 +566,14 @@
             jax.ShapeDtypeStruct((share, slots, count, orbitals), BF16),
             jax.ShapeDtypeStruct((3, count, atoms), F32),
         ),
-        in_specs=[smem, vmem, vmem, pl.BlockSpec(memory_space=pl.ANY)],
+        in_specs=[pl.BlockSpec(memory_space=pl.ANY)] * 3,
         out_specs=(vmem, vmem),
         scratch_shapes=[
             pltpu.SMEM((count, slots), jnp.int32),
+            pltpu.SMEM((count, slots), jnp.int32),
             pltpu.SMEM((count, slots), F32),
+            pltpu.VMEM((count, slots), jnp.int32),
+            pltpu.VMEM((3, 3, count, atoms), BF16),
             pltpu.VMEM((count, 3, atoms, orbitals), F32),
             pltpu.VMEM((3 * count, span, orbitals), BF16),
             pltpu.VMEM((peers, 3 * count, span, orbitals), BF16),
@@ -532,18 +581,20 @@
             pltpu.VMEM((count, orbitals, slots * orbitals), F32),
             pltpu.VMEM((count, orbitals, slots * orbitals), BF16),
             pltpu.VMEM((count, slots, 7, atoms, orbitals), F32),
-            pltpu.VMEM((space, 8, LANES), F32),
+            pltpu.VMEM((steps, 8, LANES), F32),
+            pltpu.VMEM((steps, 8, LANES), F32),
+            pltpu.VMEM((count, slots, 3, share, orbitals), F32),
             pltpu.VMEM((count, orbitals, span), F32),
             pltpu.VMEM((3 * count, orbitals, span), BF16),
             pltpu.VMEM((count, orbitals, span), BF16),
             pltpu.VMEM((wide, count, share, span), BF16),
             pltpu.VMEM((3 * count, count, share, orbitals), F32),
             pltpu.VMEM((share * count, orbitals), F32),
-            pltpu.VMEM((slots, 3, 8, orbitals), F32),
+            pltpu.VMEM((count, -(-slots // 8) * 8, 3, 8, orbitals), F32),
+            pltpu.VMEM((3, count, min(atoms, share), orbitals), F32),
             pltpu.VMEM((3, 3 * count, orbitals), F32),
-            pltpu.VMEM((3, count, orbitals), F32),
             pltpu.VMEM((3, wide, 3, count, orbitals), F32),
-            dma,
+            dma((4,)),
             dma((2,)),
             dma((2,)),
             dma((2,)),
@@ -554,8 +605,8 @@
             dma((peers,)),
             dma((peers,)),
             dma((peers,)),
-            dma((space,)),
-            dma((space,)),
+            dma((steps,)),
+            dma((steps,)),
             dma((2, count)),
             dma((2, count)),
             dma((peers, count)),
@@ -566,7 +617,7 @@
         compiler_params=pltpu.CompilerParams(
             collective_id=0, has_side_effects=True, vmem_limit_bytes=60 * 1024 * 1024
         ),
-    )(neighbours, neighbours, jnp.transpose(positions, (1, 0, 2)), probes)
+    )(neighbours, jnp.transpose(positions, (1, 0, 2)), probes)
     return jnp.transpose(density, (0, 2, 1, 3)), jnp.transpose(force, (1, 0, 2))
 
 

time: 61.3 us -> 52.9 us (0.86)
  Pallas kernels: 56.9 us -> 48.6 us
    pallas_call x1, Pallas kernels: 56.9 us -> 48.6 us  [per_device(): pl.pallas_call(functools.partial(kernel, sizes), name='band_forces', out_...]
where the time goes in v1:
time: 52.9 us; the launch traced here: 52.8 us
  Pallas kernels  48.6 us (92%)
  local copies, waits for them, and re-layouts  3.57 us (7%)
  between operations  0.65 us (1%)
    pallas_call x1, Pallas kernels, per_device(): pl.pallas_call(functools.partial(kernel, sizes), name='band_forces', out_...  48.6 us
    unnamed x4, local copies, waits for them, and re-layouts  3.57 us

profile of v1, /device:TPU:0, one launch (start us, length us, event | category | flops | bytes accessed | tf_op | source)
XLA Modules:
  0.0 52.8 jit_solution(8736328132668484035)
XLA Ops:
  0.6 48.6 %band_forces.1 = (bf16[64,15,8,128]{3,2,1,0:T(8,128)(2,1)}, f32[3,8,32]{2,1,0:T(8,128)}) custom-call(s32[8,15]{1,0:T(8,128)} %neighbours_ref.1, bf16[3,8,32]{2,1,0:T(8,128)(2,1)} %bitcast.5, bf16[8,256,128]{2,1,0:T(8,128)(2,1)} %probes_ref.1), custom_call_target="tpu_custom_call" | custom-call | tf_op jit(solution)/shard_map/band_forces/pallas_call | solution.py:562
  49.2 0.0 copy-start
  49.2 3.0 %copy.7 = bf16[64,8,15,128]{3,1,2,0:T(8,128)(2,1)} copy(bf16[64,8,15,128]{3,1,2,0:T(8,128)(2,1)} %bitcast.3) | data formatting | bytes 3932160
  52.2 0.0 copy-done
  52.2 0.6 %copy.8 = f32[8,3,32]{2,0,1:T(8,128)} copy(f32[8,3,32]{2,0,1:T(8,128)S(1)} %bitcast.4) | data formatting | bytes 6144
Async XLA Ops:
  49.2 3.0 %copy-start = (f32[3,8,32]{2,1,0:T(8,128)S(1)}, f32[3,8,32]{2,1,0:T(8,128)}, u32[]{:S(2)}) copy-start(f32[3,8,32]{2,1,0:T(8,128)} %get-tuple-element.5) | copy-start | bytes 9220

commit v2 on v1

--- a/solution.py
+++ b/solution.py
@@ -40,6 +40,7 @@
 
 
 SHIFTS = offsets()
+PIECES = 8
 
 
 def kernel(
@@ -546,6 +547,18 @@
         copy.wait_send()
 
 
+def write_out(pieces, dens_in, force_in, dens_out, force_out, sems):
+    rows = dens_in.shape[0] // pieces
+    copies = [pltpu.make_async_copy(force_in, force_out, sems.at[pieces])]
+    for i in range(pieces):
+        part = pl.ds(i * rows, rows)
+        copies.append(pltpu.make_async_copy(dens_in.at[part], dens_out.at[part], sems.at[i]))
+    for copy in copies:
+        copy.start()
+    for copy in copies:
+        copy.wait()
+
+
 def per_device(positions, probes, neighbours):
     count, _, atoms = positions.shape
     slots = neighbours.shape[1]
@@ -563,8 +576,8 @@
         functools.partial(kernel, sizes),
         name="band_forces",
         out_shape=(
-            jax.ShapeDtypeStruct((share, slots, count, orbitals), BF16),
-            jax.ShapeDtypeStruct((3, count, atoms), F32),
+            pltpu.VMEM((share, slots, count, orbitals), BF16),
+            pltpu.VMEM((3, count, atoms), F32),
         ),
         in_specs=[pl.BlockSpec(memory_space=pl.ANY)] * 3,
         out_specs=(vmem, vmem),
@@ -618,6 +631,19 @@
             collective_id=0, has_side_effects=True, vmem_limit_bytes=60 * 1024 * 1024
         ),
     )(neighbours, jnp.transpose(positions, (1, 0, 2)), probes)
+    anywhere = pl.BlockSpec(memory_space=pl.ANY)
+    density, force = pl.pallas_call(
+        functools.partial(write_out, PIECES),
+        name="write_out",
+        out_shape=(
+            jax.ShapeDtypeStruct(density.shape, BF16),
+            jax.ShapeDtypeStruct(force.shape, F32),
+        ),
+        in_specs=[vmem, vmem],
+        out_specs=(anywhere, anywhere),
+        scratch_shapes=[dma((PIECES + 1,))],
+        compiler_params=pltpu.CompilerParams(vmem_limit_bytes=1024 * 1024),
+    )(density, force)
     return jnp.transpose(density, (0, 2, 1, 3)), jnp.transpose(force, (1, 0, 2))
 
 

time: 52.9 us -> 49.4 us (0.934)
  local copies, waits for them, and re-layouts: 3.57 us -> 0 us
    unnamed x4 -> x0, local copies, waits for them, and re-layouts: 3.57 us -> none
    pallas_call x0 -> x1, Pallas kernels: none -> 1.34 us  [per_device(): pl.pallas_call(functools.partial(write_out, PIECES), name='write_out', ou...]
    pallas_call x1, Pallas kernels: 48.6 us -> 47.3 us  [per_device(): pl.pallas_call(functools.partial(kernel, sizes), name='band_forces', out_...]
where the time goes in v2:
time: 49.4 us; the launch traced here: 49.2 us
  Pallas kernels  48.6 us (98%)
  between operations  0.64 us (1%)
    pallas_call x1, Pallas kernels, per_device(): pl.pallas_call(functools.partial(kernel, sizes), name='band_forces', out_...  47.3 us
    pallas_call x1, Pallas kernels, per_device(): pl.pallas_call(functools.partial(write_out, PIECES), name='write_out', ou...  1.34 us

profile of v2, /device:TPU:0, one launch (start us, length us, event | category | flops | bytes accessed | tf_op | source)
XLA Modules:
  0.0 49.2 jit_solution(9101707014811898045)
XLA Ops:
  0.6 47.3 %band_forces.1 = (bf16[64,15,8,128]{3,2,1,0:T(8,128)(2,1)S(1)}, f32[3,8,32]{2,1,0:T(8,128)S(1)}) custom-call(s32[8,15]{1,0:T(8,128)} %neighbours_ref.1, bf16[3,8,32]{2,1,0:T(8,128)(2,1)} %bitcast.3, bf16[8,256,128]{2,1,0:T(8,128)(2,1)} %probes_ref.1), custom_call_target="tpu_custom_call" | custom-call | tf_op jit(solution)/shard_map/band_forces/pallas_call | solution.py:575
  47.9 1.3 %write_out.1 = (bf16[64,15,8,128]{3,2,1,0:T(8,128)(2,1)}, f32[3,8,32]{2,1,0:T(8,128)}) custom-call(bf16[64,15,8,128]{3,2,1,0:T(8,128)(2,1)S(1)} %get-tuple-element.6.dens_in, f32[3,8,32]{2,1,0:T(8,128)S(1)} %get-tuple-element.7.force_in), custom_call_target="tpu_custom_call" | custom-call | tf_op jit(solution)/shard_map/write_out/pallas_call | solution.py:635

commit v3 on v2

--- a/solution.py
+++ b/solution.py
@@ -41,6 +41,8 @@
 
 SHIFTS = offsets()
 PIECES = 8
+EARLY_BUILD = 3
+EARLY_SLOPES = 2
 
 
 def kernel(
@@ -95,7 +97,8 @@
     pull_s,
     pull_r,
 ):
-    space, wide, count, atoms, slots, span, share = sizes
+    space, wide, count, atoms, slots, span, share, chunks, plane = sizes
+    width = span // chunks
     orbitals = 4 * atoms
     total = span * wide
     s = lax.axis_index("space")
@@ -117,11 +120,10 @@
             device_id_type=MESH,
         )
 
-    steps = space.bit_length() - 1
-    partners = []
-    for j in range(steps):
-        bit = lax.rem(lax.div(s, 2**j), 2)
-        partners.append(s + 2**j * (1 - 2 * bit))
+    low, high = lax.rem(s, plane), lax.div(s, plane)
+    planes = space // plane
+    beside = [high * plane + lax.rem(low + d, plane) for d in range(1, plane)]
+    across = [lax.rem(high + d, planes) * plane + low for d in range(1, planes)]
 
     barrier = pltpu.get_barrier_semaphore()
 
@@ -133,7 +135,7 @@
             device_id_type=MESH,
         )
 
-    for to in partners + [up, down]:
+    for to in beside + across + [up, down]:
         greet(to, q)
     for e in range(1, wide):
         for to in (s, up, down):
@@ -146,34 +148,60 @@
                 (positions_ref, raw_pos.at[1]),
                 (neighbours_ref, names_ref),
                 (neighbours_ref, wanted_ref),
-                (probes_ref, near.at[own]),
+            ]
+            + [
+                (probes_ref.at[:, pl.ds(j * width, width)], near[j].at[own])
+                for j in range(chunks)
             ]
         )
     ]
     for load in loads:
         load.start()
-    pl.semaphore_wait(barrier, steps + 2 + 3 * (wide - 1))
+    pl.semaphore_wait(barrier, plane + planes + 3 * (wide - 1))
 
     pos_up = send(positions_ref, raw_pos.at[0], pos_s.at[0], pos_r.at[0], up, q)
     pos_down = send(positions_ref, raw_pos.at[2], pos_s.at[1], pos_r.at[1], down, q)
     pos_up.start()
     pos_down.start()
-    probe_up = send(probes_ref, near.at[before], probe_s.at[0], probe_r.at[0], up, q)
-    probe_down = send(probes_ref, near.at[after], probe_s.at[1], probe_r.at[1], down, q)
-    probe_up.start()
-    probe_down.start()
-    own_out = []
-    for e in range(1, wide):
-        copy = send(
-            probes_ref,
-            rest.at[e - 1, own],
-            own_s.at[e - 1],
-            own_r.at[e - 1],
-            s,
-            lax.rem(q + e, wide),
-        )
-        copy.start()
-        own_out.append(copy)
+    def probe_copies(j):
+        part = pl.ds(j * width, width)
+        return [
+            send(
+                probes_ref.at[:, part],
+                near[j].at[place],
+                probe_s.at[i, j],
+                probe_r.at[i, j],
+                to,
+                q,
+            )
+            for i, (place, to) in enumerate([(before, up), (after, down)])
+        ]
+
+    crossing = jnp.logical_or(lax.rem(s, 4) == 0, lax.rem(s, 4) == 3)
+
+    def start_probes(j, when):
+        @pl.when(when)
+        def _():
+            for copy in probe_copies(j):
+                copy.start()
+
+    start_probes(0, jnp.logical_not(crossing))
+    def own_copies(j):
+        return [
+            send(
+                probes_ref.at[:, pl.ds(j * width, width)],
+                rest[j].at[e - 1, own],
+                own_s.at[e - 1, j],
+                own_r.at[e - 1, j],
+                s,
+                lax.rem(q + e, wide),
+            )
+            for e in range(1, wide)
+        ]
+
+    for j in range(chunks):
+        for copy in own_copies(j):
+            copy.start()
 
     def fold(x):
         return (
@@ -209,6 +237,7 @@
         return carry
 
     lax.fori_loop(0, count, find_slots, 0)
+    start_probes(0, crossing)
     pos_up.wait_recv()
     spread(0)
     pos_down.wait_recv()
@@ -278,75 +307,6 @@
             pair[c, k, 6] = g * (square * inv) * (2.0 / (BOND_LENGTH * BOND_LENGTH))
         return carry
 
-    peak = lax.fori_loop(0, count, peak_of, jnp.zeros((atoms, 1), F32))
-    top = jnp.broadcast_to(jnp.max(peak, axis=0, keepdims=True), (8, LANES))
-    order = [0] + list(range(2, steps)) + ([1] if steps > 1 else [])
-    done = 0
-    for t, j in enumerate(order):
-        top_out[j] = top
-        copy = send(top_out.at[j], top_in.at[j], max_s.at[j], max_r.at[j], partners[j], q)
-        copy.start()
-        until = count if t == len(order) - 1 else count * (t + 1) // len(order)
-        lax.fori_loop(done, until, build, 0)
-        done = until
-        copy.wait()
-        top = jnp.maximum(top, top_in[j])
-    shrink = 1.0 / top[0:1]
-
-    loads[3].wait()
-    probe_up.wait_recv()
-    probe_down.wait_recv()
-    fwd_out = []
-    for e in range(1, wide):
-        copy = send(
-            near.at[far_side],
-            rest.at[e - 1, far_side],
-            fwd_s.at[e - 1],
-            fwd_r.at[e - 1],
-            s,
-            lax.rem(q + e, wide),
-        )
-        copy.start()
-        fwd_out.append(copy)
-
-    def one_copies(c):
-        return (
-            send(one_t.at[count + c], one_t.at[c], one_s.at[0, c], one_r.at[0, c], up, q),
-            send(
-                one_t.at[count + c], one_t.at[2 * count + c], one_s.at[1, c], one_r.at[1, c], down, q
-            ),
-        )
-
-    def term_one(c, carry):
-        for k in range(slots):
-            part = pl.ds(k * orbitals, orbitals)
-            scaled[c, :, part] = (ham[c, :, part] * shrink).astype(BF16)
-        right = jnp.concatenate([near[slot_ref[c, k]] for k in range(slots)], axis=1)
-        term = lax.dot_general(
-            scaled[c], right, (((1,), (1,)), ((), ())), preferred_element_type=F32
-        )
-        first[c] = term
-        one_t[count + c] = term.astype(BF16)
-        for copy in one_copies(c):
-            copy.start()
-        return carry
-
-    lax.fori_loop(0, count, term_one, 0)
-
-    chip_out = []
-    for e in range(1, wide):
-        own_out[e - 1].wait_recv()
-        copy = send(
-            rest.at[e - 1, own],
-            rest.at[e - 1, far_side],
-            chip_s.at[e - 1],
-            chip_r.at[e - 1],
-            mate,
-            q,
-        )
-        copy.start()
-        chip_out.append(copy)
-
     height = min(atoms, share)
     turns = share // height
     start_atom = lax.rem(q * share, atoms)
@@ -381,14 +341,135 @@
                     )
         return carry
 
-    lax.fori_loop(0, count, slopes, 0)
-
-    def wait_one(c, carry):
-        for copy in one_copies(c):
+    peak = lax.fori_loop(0, count, peak_of, jnp.zeros((atoms, 1), F32))
+    top = jnp.broadcast_to(jnp.max(peak, axis=0, keepdims=True), (8, LANES))
+
+    def top_copies(stage, devices):
+        base = 0 if stage == 0 else plane - 1
+        return [
+            send(
+                top_out.at[stage],
+                top_in.at[base + i],
+                max_s.at[base + i],
+                max_r.at[base + i],
+                to,
+                q,
+            )
+            for i, to in enumerate(devices)
+        ]
+
+    def raise_top(top, stage, devices):
+        base = 0 if stage == 0 else plane - 1
+        for i, copy in enumerate(top_copies(stage, devices)):
             copy.wait()
+            top = jnp.maximum(top, top_in[base + i])
+        return top
+
+    def forward(j):
+        copies = []
+        for e in range(1, wide):
+            copies.append(
+                send(
+                    near[j].at[far_side],
+                    rest[j].at[e - 1, far_side],
+                    fwd_s.at[e - 1, j],
+                    fwd_r.at[e - 1, j],
+                    s,
+                    lax.rem(q + e, wide),
+                )
+            )
+        return copies
+
+    top_out[0] = top
+    for copy in top_copies(0, beside):
+        copy.start()
+    for j in range(1, chunks):
+        start_probes(j, jnp.logical_not(crossing))
+    lax.fori_loop(0, EARLY_BUILD, build, 0)
+    top = raise_top(top, 0, beside)
+    top_out[1] = top
+    for copy in top_copies(1, across):
+        copy.start()
+    for j in range(1, chunks):
+        start_probes(j, crossing)
+    lax.fori_loop(EARLY_BUILD, count, build, 0)
+    lax.fori_loop(0, EARLY_SLOPES, slopes, 0)
+    for load in loads[3:]:
+        load.wait()
+    for copy in probe_copies(0):
+        copy.wait_recv()
+    for copy in forward(0):
+        copy.start()
+    top = raise_top(top, 1, across)
+    shrink = 1.0 / top[0:1]
+
+    def one_copies(j, c):
+        return [
+            send(
+                one_t[j].at[count + c],
+                one_t[j].at[place + c],
+                one_s.at[i, j, c],
+                one_r.at[i, j, c],
+                to,
+                q,
+            )
+            for i, (place, to) in enumerate([(0, up), (2 * count, down)])
+        ]
+
+    def term_one(j):
+        def body(c, carry):
+            right = jnp.concatenate([near[j][slot_ref[c, k]] for k in range(slots)], axis=1)
+            term = lax.dot_general(
+                scaled[c], right, (((1,), (1,)), ((), ())), preferred_element_type=F32
+            )
+            first[j, c] = term
+            one_t[j][count + c] = term.astype(BF16)
+            for copy in one_copies(j, c):
+                copy.start()
+            return carry
+
+        lax.fori_loop(0, count, body, 0)
+
+    def scale_down(c, carry):
+        for k in range(slots):
+            here = pl.ds(k * orbitals, orbitals)
+            scaled[c, :, here] = (ham[c, :, here] * shrink).astype(BF16)
         return carry
 
-    lax.fori_loop(0, count, wait_one, 0)
+    lax.fori_loop(0, count, scale_down, 0)
+    term_one(0)
+    def later_slopes(when):
+        @pl.when(when)
+        def _():
+            lax.fori_loop(EARLY_SLOPES, count, slopes, 0)
+
+    for j in range(1, chunks):
+        for copy in probe_copies(j):
+            copy.wait_recv()
+        for copy in forward(j):
+            copy.start()
+    later_slopes(crossing)
+    for j in range(1, chunks):
+        term_one(j)
+    later_slopes(jnp.logical_not(crossing))
+
+    def mate_copies(j):
+        return [
+            send(
+                rest[j].at[e - 1, own],
+                rest[j].at[e - 1, far_side],
+                chip_s.at[e - 1, j],
+                chip_r.at[e - 1, j],
+                mate,
+                q,
+            )
+            for e in range(1, wide)
+        ]
+
+    for j in range(chunks):
+        for copy, onward in zip(own_copies(j), mate_copies(j)):
+            copy.wait_recv()
+            onward.start()
 
     eye = (
         lax.broadcasted_iota(jnp.int32, (orbitals, orbitals), 0)
@@ -396,71 +477,80 @@
     ).astype(BF16)
     my_rows = pl.ds(pl.multiple_of(q * share, share), share)
 
-    def mix_copies(c):
+    def mix_copies(j, c):
         copies = []
         for e in range(1, wide):
             to = lax.rem(q + e, wide)
             copies.append(
                 send(
-                    mix.at[c, pl.ds(pl.multiple_of(to * share, share), share)],
-                    row_mix.at[q, c],
-                    mix_s.at[e - 1, c],
-                    mix_r.at[e - 1, c],
+                    mix.at[j, c, pl.ds(pl.multiple_of(to * share, share), share)],
+                    row_mix.at[j, q, c],
+                    mix_s.at[e - 1, j, c],
+                    mix_r.at[e - 1, j, c],
                     s,
                     to,
                 )
             )
         return copies
 
-    def term_two(c, carry):
-        right = jnp.concatenate([one_t[slot_ref[c, k]] for k in range(slots)], axis=0)
-        term = jnp.dot(scaled[c], right, preferred_element_type=F32)
-        probe = lax.dot_general(
-            eye, near[count + c], (((1,), (1,)), ((), ())), preferred_element_type=F32
-        )
-        second = 2.0 * term - probe
-        mix[c] = (COEFF_ZERO * probe + COEFF_ONE * first[c] + COEFF_TWO * second).astype(BF16)
-        row_mix[q, c] = mix[c, my_rows, :]
-        for copy in mix_copies(c):
-            copy.start()
-        return carry
-
-    lax.fori_loop(0, count, term_two, 0)
-
-    def product(w, t):
-        left = row_mix[lax.rem(q + wide - w, wide)].reshape(count * share, span)
-        source = near if w == 0 else rest.at[w - 1]
-        right = jnp.concatenate([source[2 * t], source[2 * t + 1]], axis=1)
-        part = jnp.dot(left, right, preferred_element_type=F32)
-        return [
-            part[:, h * orbitals : (h + 1) * orbitals].reshape(count, share, orbitals)
-            for h in range(2)
-        ]
-
-    def overlap_own(t, carry):
-        dense[2 * t], dense[2 * t + 1] = product(0, t)
-        return carry
-
-    lax.fori_loop(0, 3 * count // 2, overlap_own, 0)
-
-    for copy in fwd_out + chip_out:
-        copy.wait_recv()
-
-    def wait_mix(c, carry):
-        for copy in mix_copies(c):
-            copy.wait()
-        return carry
-
-    lax.fori_loop(0, count, wait_mix, 0)
-
-    def overlap_rest(t, carry):
-        for w in range(1, wide):
-            low, high = product(w, t)
-            dense[2 * t] = dense[2 * t] + low
-            dense[2 * t + 1] = dense[2 * t + 1] + high
-        return carry
-
-    lax.fori_loop(0, 3 * count // 2, overlap_rest, 0)
+    def term_two(j):
+        def wait_one(c, carry):
+            for copy in one_copies(j, c):
+                copy.wait()
+            return carry
+
+        def body(c, carry):
+            right = jnp.concatenate([one_t[j][slot_ref[c, k]] for k in range(slots)], axis=0)
+            term = jnp.dot(scaled[c], right, preferred_element_type=F32)
+            probe = lax.dot_general(
+                eye, near[j][count + c], (((1,), (1,)), ((), ())), preferred_element_type=F32
+            )
+            second = 2.0 * term - probe
+            mix[j, c] = (
+                COEFF_ZERO * probe + COEFF_ONE * first[j, c] + COEFF_TWO * second
+            ).astype(BF16)
+            row_mix[j, q, c] = mix[j, c, my_rows, :]
+            for copy in mix_copies(j, c):
+                copy.start()
+            return carry
+
+        lax.fori_loop(0, count, wait_one, 0)
+        lax.fori_loop(0, count, body, 0, unroll=4)
+
+    def overlap(j):
+        def wait_mix(c, carry):
+            for copy in mix_copies(j, c):
+                copy.wait()
+            return carry
+
+        def body(t, carry):
+            left = jnp.concatenate(
+                [row_mix[j, lax.rem(q + wide - w, wide)] for w in range(wide)], axis=2
+            ).reshape(count * share, wide * width)
+            right = jnp.concatenate(
+                [
+                    jnp.concatenate([source[2 * t], source[2 * t + 1]], axis=1)
+                    for source in [near[j]] + [rest[j].at[w - 1] for w in range(1, wide)]
+                ],
+                axis=0,
+            )
+            product = jnp.dot(left, right, preferred_element_type=F32)
+            for h in range(2):
+                value = product[:, h * orbitals : (h + 1) * orbitals].reshape(
+                    count, share, orbitals
+                )
+                dense[2 * t + h] = value if j == 0 else dense[2 * t + h] + value
+            return carry
+
+        for copy in forward(j) + mate_copies(j):
+            copy.wait_recv()
+        lax.fori_loop(0, count, wait_mix, 0)
+        lax.fori_loop(0, 3 * count // 2, body, 0, unroll=4)
+
+    for j in range(chunks):
+        term_two(j)
+    for j in range(chunks):
+        overlap(j)
 
     padded = col_force.shape[1]
 
@@ -543,7 +633,10 @@
             result = part if result is None else result + part
     force_ref[...] = (result * (-1.0 / total))[:, :, :atoms]
 
-    for copy in [pos_up, pos_down, probe_up, probe_down] + own_out + fwd_out + chip_out:
+    sent = [pos_up, pos_down]
+    for j in range(chunks):
+        sent = sent + probe_copies(j) + own_copies(j) + forward(j) + mate_copies(j)
+    for copy in sent:
         copy.wait_send()
 
 
@@ -567,11 +660,14 @@
     space = lax.axis_size("space")
     wide = lax.axis_size("probe")
     share = orbitals // wide
-    sizes = (space, wide, count, atoms, slots, span, share)
     vmem = pl.BlockSpec(memory_space=pltpu.VMEM)
     dma = pltpu.SemaphoreType.DMA
     peers = max(wide - 1, 1)
-    steps = space.bit_length() - 1
+    chunks = 2 if span % (2 * LANES) == 0 else 1
+    plane = 2 ** ((space.bit_length() - 1) // 2)
+    pairs = plane + space // plane - 2
+    width = span // chunks
+    sizes = (space, wide, count, atoms, slots, span, share, chunks, plane)
     density, force = pl.pallas_call(
         functools.partial(kernel, sizes),
         name="band_forces",
@@ -588,42 +684,42 @@
             pltpu.VMEM((count, slots), jnp.int32),
             pltpu.VMEM((3, 3, count, atoms), BF16),
             pltpu.VMEM((count, 3, atoms, orbitals), F32),
-            pltpu.VMEM((3 * count, span, orbitals), BF16),
-            pltpu.VMEM((peers, 3 * count, span, orbitals), BF16),
+            [pltpu.VMEM((3 * count, width, orbitals), BF16)] * chunks,
+            [pltpu.VMEM((peers, 3 * count, width, orbitals), BF16)] * chunks,
             pltpu.VMEM((3, 3 * count, orbitals), F32),
             pltpu.VMEM((count, orbitals, slots * orbitals), F32),
             pltpu.VMEM((count, orbitals, slots * orbitals), BF16),
             pltpu.VMEM((count, slots, 7, atoms, orbitals), F32),
-            pltpu.VMEM((steps, 8, LANES), F32),
-            pltpu.VMEM((steps, 8, LANES), F32),
+            pltpu.VMEM((2, 8, LANES), F32),
+            pltpu.VMEM((pairs, 8, LANES), F32),
             pltpu.VMEM((count, slots, 3, share, orbitals), F32),
-            pltpu.VMEM((count, orbitals, span), F32),
-            pltpu.VMEM((3 * count, orbitals, span), BF16),
-            pltpu.VMEM((count, orbitals, span), BF16),
-            pltpu.VMEM((wide, count, share, span), BF16),
+            pltpu.VMEM((chunks, count, orbitals, width), F32),
+            [pltpu.VMEM((3 * count, orbitals, width), BF16)] * chunks,
+            pltpu.VMEM((chunks, count, orbitals, width), BF16),
+            pltpu.VMEM((chunks, wide, count, share, width), BF16),
             pltpu.VMEM((3 * count, count, share, orbitals), F32),
             pltpu.VMEM((share * count, orbitals), F32),
             pltpu.VMEM((count, -(-slots // 8) * 8, 3, 8, orbitals), F32),
             pltpu.VMEM((3, count, min(atoms, share), orbitals), F32),
             pltpu.VMEM((3, 3 * count, orbitals), F32),
             pltpu.VMEM((3, wide, 3, count, orbitals), F32),
-            dma((4,)),
+            dma((3 + chunks,)),
             dma((2,)),
             dma((2,)),
-            dma((2,)),
-            dma((2,)),
-            dma((peers,)),
-            dma((peers,)),
-            dma((peers,)),
-            dma((peers,)),
-            dma((peers,)),
-            dma((peers,)),
-            dma((steps,)),
-            dma((steps,)),
-            dma((2, count)),
-            dma((2, count)),
-            dma((peers, count)),
-            dma((peers, count)),
+            dma((2, chunks)),
+            dma((2, chunks)),
+            dma((peers, chunks)),
+            dma((peers, chunks)),
+            dma((peers, chunks)),
+            dma((peers, chunks)),
+            dma((peers, chunks)),
+            dma((peers, chunks)),
+            dma((pairs,)),
+            dma((pairs,)),
+            dma((2, chunks, count)),
+            dma((2, chunks, count)),
+            dma((peers, chunks, count)),
+            dma((peers, chunks, count)),
             dma((3, wide)),
             dma((3, wide)),
         ],

time: 49.4 us -> 46.7 us (0.945)
  Pallas kernels: 48.6 us -> 45.9 us
    pallas_call x1, Pallas kernels: 47.3 us -> 44.6 us  [per_device(): pl.pallas_call(functools.partial(kernel, sizes), name='band_forces', out_...]
where the time goes in v3:
time: 46.7 us; the launch traced here: 46.6 us
  Pallas kernels  45.9 us (98%)
  between operations  0.64 us (1%)
    pallas_call x1, Pallas kernels, per_device(): pl.pallas_call(functools.partial(kernel, sizes), name='band_forces', out_...  44.6 us
    pallas_call x1, Pallas kernels, per_device(): pl.pallas_call(functools.partial(write_out, PIECES), name='write_out', ou...  1.34 us

profile of v3, /device:TPU:0, one launch (start us, length us, event | category | flops | bytes accessed | tf_op | source)
XLA Modules:
  0.0 46.6 jit_solution(11213241941797479351)
XLA Ops:
  0.6 44.6 %band_forces.1 = (bf16[64,15,8,128]{3,2,1,0:T(8,128)(2,1)S(1)}, f32[3,8,32]{2,1,0:T(8,128)S(1)}) custom-call(s32[8,15]{1,0:T(8,128)} %neighbours_ref.1, bf16[3,8,32]{2,1,0:T(8,128)(2,1)} %bitcast.3, bf16[8,256,128]{2,1,0:T(8,128)(2,1)} %probes_ref.1), custom_call_target="tpu_custom_call" | custom-call | tf_op jit(solution)/shard_map/band_forces/pallas_call | solution.py:671
  45.2 1.3 %write_out.1 = (bf16[64,15,8,128]{3,2,1,0:T(8,128)(2,1)}, f32[3,8,32]{2,1,0:T(8,128)}) custom-call(bf16[64,15,8,128]{3,2,1,0:T(8,128)(2,1)S(1)} %get-tuple-element.6.dens_in, f32[3,8,32]{2,1,0:T(8,128)S(1)} %get-tuple-element.7.force_in), custom_call_target="tpu_custom_call" | custom-call | tf_op jit(solution)/shard_map/write_out/pallas_call | solution.py:731

commit v4 on v3

--- a/solution.py
+++ b/solution.py
@@ -88,6 +88,8 @@
     fwd_r,
     chip_s,
     chip_r,
+    yonder_s,
+    yonder_r,
     max_s,
     max_r,
     one_s,
@@ -138,8 +140,7 @@
     for to in beside + across + [up, down]:
         greet(to, q)
     for e in range(1, wide):
-        for to in (s, up, down):
-            greet(to, lax.rem(q + e, wide))
+        greet(s, lax.rem(q + e, wide))
 
     loads = [
         pltpu.make_async_copy(src, dst, local_sem.at[i])
@@ -157,35 +158,38 @@
     ]
     for load in loads:
         load.start()
-    pl.semaphore_wait(barrier, plane + planes + 3 * (wide - 1))
+    pl.semaphore_wait(barrier, plane + planes + wide - 1)
 
     pos_up = send(positions_ref, raw_pos.at[0], pos_s.at[0], pos_r.at[0], up, q)
     pos_down = send(positions_ref, raw_pos.at[2], pos_s.at[1], pos_r.at[1], down, q)
     pos_up.start()
     pos_down.start()
-    def probe_copies(j):
+    half = count // 2
+
+    def probe_copies(j, halves=(0, 1)):
         part = pl.ds(j * width, width)
         return [
             send(
-                probes_ref.at[:, part],
-                near[j].at[place],
-                probe_s.at[i, j],
-                probe_r.at[i, j],
+                probes_ref.at[pl.ds(h * half, half), part],
+                near[j].at[pl.ds(place + h * half, half)],
+                probe_s.at[i, j, h],
+                probe_r.at[i, j, h],
                 to,
                 q,
             )
-            for i, (place, to) in enumerate([(before, up), (after, down)])
+            for i, (place, to) in enumerate([(0, up), (2 * count, down)])
+            for h in halves
         ]
 
     crossing = jnp.logical_or(lax.rem(s, 4) == 0, lax.rem(s, 4) == 3)
 
-    def start_probes(j, when):
+    def start_probes(when, j, halves=(0, 1)):
         @pl.when(when)
         def _():
-            for copy in probe_copies(j):
+            for copy in probe_copies(j, halves):
                 copy.start()
 
-    start_probes(0, jnp.logical_not(crossing))
+    start_probes(jnp.logical_not(crossing), 0, (0,))
     def own_copies(j):
         return [
             send(
@@ -237,7 +241,7 @@
         return carry
 
     lax.fori_loop(0, count, find_slots, 0)
-    start_probes(0, crossing)
+    start_probes(crossing, 0)
     pos_up.wait_recv()
     spread(0)
     pos_down.wait_recv()
@@ -341,7 +345,7 @@
                     )
         return carry
 
-    peak = lax.fori_loop(0, count, peak_of, jnp.zeros((atoms, 1), F32))
+    peak = lax.fori_loop(0, count, peak_of, jnp.zeros((atoms, 1), F32), unroll=2)
     top = jnp.broadcast_to(jnp.max(peak, axis=0, keepdims=True), (8, LANES))
 
     def top_copies(stage, devices):
@@ -365,13 +369,16 @@
             top = jnp.maximum(top, top_in[base + i])
         return top
 
+    last = chunks - 1
+
     def forward(j):
         copies = []
+        far_part = pl.ds(core * (2 * count), half if j == last else count)
         for e in range(1, wide):
             copies.append(
                 send(
-                    near[j].at[far_side],
-                    rest[j].at[e - 1, far_side],
+                    near[j].at[far_part],
+                    rest[j].at[e - 1, far_part],
                     fwd_s.at[e - 1, j],
                     fwd_r.at[e - 1, j],
                     s,
@@ -383,15 +390,16 @@
     top_out[0] = top
     for copy in top_copies(0, beside):
         copy.start()
+    start_probes(jnp.logical_not(crossing), 0, (1,))
     for j in range(1, chunks):
-        start_probes(j, jnp.logical_not(crossing))
+        start_probes(jnp.logical_not(crossing), j)
     lax.fori_loop(0, EARLY_BUILD, build, 0)
     top = raise_top(top, 0, beside)
     top_out[1] = top
     for copy in top_copies(1, across):
         copy.start()
     for j in range(1, chunks):
-        start_probes(j, crossing)
+        start_probes(crossing, j)
     lax.fori_loop(EARLY_BUILD, count, build, 0)
     lax.fori_loop(0, EARLY_SLOPES, slopes, 0)
     for load in loads[3:]:
@@ -418,6 +426,10 @@
 
     def term_one(j):
         def body(c, carry):
+            if j == 0:
+                for k in range(slots):
+                    here = pl.ds(k * orbitals, orbitals)
+                    scaled[c, :, here] = (ham[c, :, here] * shrink).astype(BF16)
             right = jnp.concatenate([near[j][slot_ref[c, k]] for k in range(slots)], axis=1)
             term = lax.dot_general(
                 scaled[c], right, (((1,), (1,)), ((), ())), preferred_element_type=F32
@@ -430,13 +442,6 @@
 
         lax.fori_loop(0, count, body, 0)
 
-    def scale_down(c, carry):
-        for k in range(slots):
-            here = pl.ds(k * orbitals, orbitals)
-            scaled[c, :, here] = (ham[c, :, here] * shrink).astype(BF16)
-        return carry
-
-    lax.fori_loop(0, count, scale_down, 0)
     term_one(0)
     def later_slopes(when):
         @pl.when(when)
@@ -465,6 +470,19 @@
             )
             for e in range(1, wide)
         ]
+
+    far_to = core * up + (1 - core) * down
+    yonder = [
+        send(
+            rest[last].at[e - 1, pl.ds(count + half, half)],
+            rest[last].at[e - 1, pl.ds((1 - core) * (2 * count) + half, half)],
+            yonder_s.at[e - 1],
+            yonder_r.at[e - 1],
+            far_to,
+            q,
+        )
+        for e in range(1, wide)
+    ]
 
     for j in range(chunks):
         for copy, onward in zip(own_copies(j), mate_copies(j)):
@@ -515,6 +533,9 @@
             return carry
 
         lax.fori_loop(0, count, wait_one, 0)
+        if j == last:
+            for copy in yonder:
+                copy.start()
         lax.fori_loop(0, count, body, 0, unroll=4)
 
     def overlap(j):
@@ -542,7 +563,7 @@
                 dense[2 * t + h] = value if j == 0 else dense[2 * t + h] + value
             return carry
 
-        for copy in forward(j) + mate_copies(j):
+        for copy in forward(j) + mate_copies(j) + (yonder if j == last else []):
             copy.wait_recv()
         lax.fori_loop(0, count, wait_mix, 0)
         lax.fori_loop(0, 3 * count // 2, body, 0, unroll=4)
@@ -633,7 +654,7 @@
             result = part if result is None else result + part
     force_ref[...] = (result * (-1.0 / total))[:, :, :atoms]
 
-    sent = [pos_up, pos_down]
+    sent = [pos_up, pos_down] + yonder
     for j in range(chunks):
         sent = sent + probe_copies(j) + own_copies(j) + forward(j) + mate_copies(j)
     for copy in sent:
@@ -706,14 +727,16 @@
             dma((3 + chunks,)),
             dma((2,)),
             dma((2,)),
-            dma((2, chunks)),
-            dma((2, chunks)),
+            dma((2, chunks, 2)),
+            dma((2, chunks, 2)),
             dma((peers, chunks)),
             dma((peers, chunks)),
             dma((peers, chunks)),
             dma((peers, chunks)),
             dma((peers, chunks)),
             dma((peers, chunks)),
+            dma((peers,)),
+            dma((peers,)),
             dma((pairs,)),
             dma((pairs,)),
             dma((2, chunks, count)),

time: 46.7 us -> 45.7 us (0.979)
  Pallas kernels: 45.9 us -> 44.9 us
    pallas_call x1, Pallas kernels: 44.6 us -> 43.6 us  [per_device(): pl.pallas_call(functools.partial(kernel, sizes), name='band_forces', out_...]
where the time goes in v4:
time: 45.7 us; the launch traced here: 45.5 us
  Pallas kernels  44.9 us (98%)
  between operations  0.64 us (1%)
    pallas_call x1, Pallas kernels, per_device(): pl.pallas_call(functools.partial(kernel, sizes), name='band_forces', out_...  43.6 us
    pallas_call x1, Pallas kernels, per_device(): pl.pallas_call(functools.partial(write_out, PIECES), name='write_out', ou...  1.34 us

profile of v4, /device:TPU:0, one launch (start us, length us, event | category | flops | bytes accessed | tf_op | source)
XLA Modules:
  0.0 45.5 jit_solution(393981634890396260)
XLA Ops:
  0.6 43.6 %band_forces.1 = (bf16[64,15,8,128]{3,2,1,0:T(8,128)(2,1)S(1)}, f32[3,8,32]{2,1,0:T(8,128)S(1)}) custom-call(s32[8,15]{1,0:T(8,128)} %neighbours_ref.1, bf16[3,8,32]{2,1,0:T(8,128)(2,1)} %bitcast.3, bf16[8,256,128]{2,1,0:T(8,128)(2,1)} %probes_ref.1), custom_call_target="tpu_custom_call" | custom-call | tf_op jit(solution)/shard_map/band_forces/pallas_call | solution.py:692
  44.2 1.3 %write_out.1 = (bf16[64,15,8,128]{3,2,1,0:T(8,128)(2,1)}, f32[3,8,32]{2,1,0:T(8,128)}) custom-call(bf16[64,15,8,128]{3,2,1,0:T(8,128)(2,1)S(1)} %get-tuple-element.6.dens_in, f32[3,8,32]{2,1,0:T(8,128)S(1)} %get-tuple-element.7.force_in), custom_call_target="tpu_custom_call" | custom-call | tf_op jit(solution)/shard_map/write_out/pallas_call | solution.py:754

commit v5 on v4

--- a/solution.py
+++ b/solution.py
@@ -42,7 +42,7 @@
 SHIFTS = offsets()
 PIECES = 8
 EARLY_BUILD = 3
-EARLY_SLOPES = 2
+EARLY_SLOPES = 0
 
 
 def kernel(
@@ -203,9 +203,8 @@
             for e in range(1, wide)
         ]
 
-    for j in range(chunks):
-        for copy in own_copies(j):
-            copy.start()
+    for copy in own_copies(0):
+        copy.start()
 
     def fold(x):
         return (
@@ -303,12 +302,12 @@
             parts = [coef_s * g] + [(l[m] * coef_p + pp[m]) * g for m in range(3)]
             for a in range(4):
                 ham[c, a * atoms : (a + 1) * atoms, k * orbitals : (k + 1) * orbitals] = parts[a]
-            pair[c, k, 0] = jnp.zeros_like(g)
+            pair[c, k, 0] = jnp.full_like(g, SP_SIGMA / PP_DIFF)
             for m in range(3):
                 pair[c, k, 1 + m] = l[m]
-            pair[c, k, 4] = beta
+            pair[c, k, 4] = coef_p
             pair[c, k, 5] = g * inv
-            pair[c, k, 6] = g * (square * inv) * (2.0 / (BOND_LENGTH * BOND_LENGTH))
+            pair[c, k, 6] = square * inv * (2.0 / (BOND_LENGTH * BOND_LENGTH))
         return carry
 
     height = min(atoms, share)
@@ -324,25 +323,22 @@
     def slopes(c, carry):
         for t in range(turns):
             kind = (q * share) // atoms + t
-            ws = jnp.where(kind == 0, 1.0, 0.0).astype(F32)
-            wr = [jnp.where(kind == m + 1, 1.0, 0.0).astype(F32) for m in range(3)]
-            wv = PP_PI * (wr[0] * p_mask[0] + wr[1] * p_mask[1] + wr[2] * p_mask[2])
-            wv = wv + (ws * SS_SIGMA) * s_mask
+            is_row_p = jnp.where(kind > 0, 1.0, 0.0).astype(F32)
+            plane_of = jnp.maximum(kind - 1, 0)
+            twice = (1.0 + is_row_p) * (1.0 / PP_DIFF)
+            lift = (SP_SIGMA / PP_DIFF) * s_mask
+            own_rows = pl.ds(pl.multiple_of(q * share + t * height, height), height)
+            part = slice(t * height, (t + 1) * height)
             for k in range(slots):
-                alpha = pair[c, k, kind, rows, :]
-                beta = pair[c, k, 4, rows, :]
+                c_two = pair[c, k, 4, rows, :]
                 lean = pair[c, k, 5, rows, :]
-                c_one = PP_DIFF * alpha + ws * SP_SIGMA
-                c_two = PP_DIFF * beta - SP_SIGMA * s_mask
-                cross = alpha * c_two
-                bracket = (ws * SP_SIGMA) * beta + cross + wv
-                x = lean * c_one
+                x = lean * (PP_DIFF * pair[c, k, kind, rows, :])
                 y = lean * c_two
-                drag = lean * (c_one * beta + cross) + pair[c, k, 6, rows, :] * bracket
+                block = ham[c, own_rows, k * orbitals : (k + 1) * orbitals]
+                drag = x * (c_two * twice + lift) + block * pair[c, k, 6, rows, :]
                 for m in range(3):
-                    slope[c, k, m, t * height : (t + 1) * height] = (
-                        x * p_mask[m] + y * wr[m] - drag * pair[c, k, 1 + m, rows, :]
-                    )
+                    slope[c, k, m, part] = x * p_mask[m] - drag * pair[c, k, 1 + m, rows, :]
+                slope[c, k, plane_of, part] = slope[c, k, plane_of, part] + y * is_row_p
         return carry
 
     peak = lax.fori_loop(0, count, peak_of, jnp.zeros((atoms, 1), F32), unroll=2)
@@ -393,6 +389,9 @@
     start_probes(jnp.logical_not(crossing), 0, (1,))
     for j in range(1, chunks):
         start_probes(jnp.logical_not(crossing), j)
+    for j in range(1, chunks):
+        for copy in own_copies(j):
+            copy.start()
     lax.fori_loop(0, EARLY_BUILD, build, 0)
     top = raise_top(top, 0, beside)
     top_out[1] = top

time: 45.7 us -> 45.6 us (level)
  no operation moved by 1% of the time
where the time goes in v5:
time: 45.6 us; the launch traced here: 45.4 us
  Pallas kernels  44.8 us (98%)
  between operations  0.64 us (1%)
    pallas_call x1, Pallas kernels, per_device(): pl.pallas_call(functools.partial(kernel, sizes), name='band_forces', out_...  43.4 us
    pallas_call x1, Pallas kernels, per_device(): pl.pallas_call(functools.partial(write_out, PIECES), name='write_out', ou...  1.34 us

profile of v5, /device:TPU:0, one launch (start us, length us, event | category | flops | bytes accessed | tf_op | source)
XLA Modules:
  0.0 45.4 jit_solution(2185472300786926115)
XLA Ops:
  0.6 43.4 %band_forces.1 = (bf16[64,15,8,128]{3,2,1,0:T(8,128)(2,1)S(1)}, f32[3,8,32]{2,1,0:T(8,128)S(1)}) custom-call(s32[8,15]{1,0:T(8,128)} %neighbours_ref.1, bf16[3,8,32]{2,1,0:T(8,128)(2,1)} %bitcast.3, bf16[8,256,128]{2,1,0:T(8,128)(2,1)} %probes_ref.1), custom_call_target="tpu_custom_call" | custom-call | tf_op jit(solution)/shard_map/band_forces/pallas_call | solution.py:691
  44.1 1.3 %write_out.1 = (bf16[64,15,8,128]{3,2,1,0:T(8,128)(2,1)}, f32[3,8,32]{2,1,0:T(8,128)}) custom-call(bf16[64,15,8,128]{3,2,1,0:T(8,128)(2,1)S(1)} %get-tuple-element.6.dens_in, f32[3,8,32]{2,1,0:T(8,128)S(1)} %get-tuple-element.7.force_in), custom_call_target="tpu_custom_call" | custom-call | tf_op jit(solution)/shard_map/write_out/pallas_call | solution.py:753

commit v6 on v5

--- a/solution.py
+++ b/solution.py
@@ -41,7 +41,7 @@
 
 SHIFTS = offsets()
 PIECES = 8
-EARLY_BUILD = 3
+EARLY_BUILD = 2
 EARLY_SLOPES = 0
 
 
@@ -535,7 +535,7 @@
         if j == last:
             for copy in yonder:
                 copy.start()
-        lax.fori_loop(0, count, body, 0, unroll=4)
+        lax.fori_loop(0, count, body, 0, unroll=2)
 
     def overlap(j):
         def wait_mix(c, carry):
@@ -565,7 +565,7 @@
         for copy in forward(j) + mate_copies(j) + (yonder if j == last else []):
             copy.wait_recv()
         lax.fori_loop(0, count, wait_mix, 0)
-        lax.fori_loop(0, 3 * count // 2, body, 0, unroll=4)
+        lax.fori_loop(0, 3 * count // 2, body, 0, unroll=12)
 
     for j in range(chunks):
         term_two(j)
@@ -592,7 +592,7 @@
         for c in range(count):
             for m in range(3):
                 col_force[c, k, m] = jnp.zeros((8, orbitals), F32)
-    lax.fori_loop(0, count, forces, 0)
+    lax.fori_loop(0, count, forces, 0, unroll=2)
 
     ids = lax.broadcasted_iota(jnp.int32, (3 * count, slots), 0)
     held_ids = jnp.where(

time: 45.6 us -> 45.2 us (level)
  no operation moved by 1% of the time
where the time goes in v6:
time: 45.2 us; the launch traced here: 45 us
  Pallas kernels  44.4 us (98%)
  between operations  0.64 us (1%)
    pallas_call x1, Pallas kernels, per_device(): pl.pallas_call(functools.partial(kernel, sizes), name='band_forces', out_...  43.1 us
    pallas_call x1, Pallas kernels, per_device(): pl.pallas_call(functools.partial(write_out, PIECES), name='write_out', ou...  1.34 us

profile of v6, /device:TPU:0, one launch (start us, length us, event | category | flops | bytes accessed | tf_op | source)
XLA Modules:
  0.0 45.0 jit_solution(15968717338030517673)
XLA Ops:
  0.6 43.1 %band_forces.1 = (bf16[64,15,8,128]{3,2,1,0:T(8,128)(2,1)S(1)}, f32[3,8,32]{2,1,0:T(8,128)S(1)}) custom-call(s32[8,15]{1,0:T(8,128)} %neighbours_ref.1, bf16[3,8,32]{2,1,0:T(8,128)(2,1)} %bitcast.3, bf16[8,256,128]{2,1,0:T(8,128)(2,1)} %probes_ref.1), custom_call_target="tpu_custom_call" | custom-call | tf_op jit(solution)/shard_map/band_forces/pallas_call | solution.py:691
  43.7 1.3 %write_out.1 = (bf16[64,15,8,128]{3,2,1,0:T(8,128)(2,1)}, f32[3,8,32]{2,1,0:T(8,128)}) custom-call(bf16[64,15,8,128]{3,2,1,0:T(8,128)(2,1)S(1)} %get-tuple-element.6.dens_in, f32[3,8,32]{2,1,0:T(8,128)S(1)} %get-tuple-element.7.force_in), custom_call_target="tpu_custom_call" | custom-call | tf_op jit(solution)/shard_map/write_out/pallas_call | solution.py:753

commit v7 on v6

--- a/solution.py
+++ b/solution.py
@@ -341,7 +341,7 @@
                 slope[c, k, plane_of, part] = slope[c, k, plane_of, part] + y * is_row_p
         return carry
 
-    peak = lax.fori_loop(0, count, peak_of, jnp.zeros((atoms, 1), F32), unroll=2)
+    peak = lax.fori_loop(0, count, peak_of, jnp.zeros((atoms, 1), F32), unroll=4)
     top = jnp.broadcast_to(jnp.max(peak, axis=0, keepdims=True), (8, LANES))
 
     def top_copies(stage, devices):

time: 45.2 us -> 45.4 us (level)
  no operation moved by 1% of the time
where the time goes in v7:
time: 45.4 us; the launch traced here: 45.2 us
  Pallas kernels  44.6 us (98%)
  between operations  0.64 us (1%)
    pallas_call x1, Pallas kernels, per_device(): pl.pallas_call(functools.partial(kernel, sizes), name='band_forces', out_...  43.2 us
    pallas_call x1, Pallas kernels, per_device(): pl.pallas_call(functools.partial(write_out, PIECES), name='write_out', ou...  1.34 us

profile of v7, /device:TPU:0, one launch (start us, length us, event | category | flops | bytes accessed | tf_op | source)
XLA Modules:
  0.0 45.2 jit_solution(3631976087393307398)
XLA Ops:
  0.6 43.2 %band_forces.1 = (bf16[64,15,8,128]{3,2,1,0:T(8,128)(2,1)S(1)}, f32[3,8,32]{2,1,0:T(8,128)S(1)}) custom-call(s32[8,15]{1,0:T(8,128)} %neighbours_ref.1, bf16[3,8,32]{2,1,0:T(8,128)(2,1)} %bitcast.3, bf16[8,256,128]{2,1,0:T(8,128)(2,1)} %probes_ref.1), custom_call_target="tpu_custom_call" | custom-call | tf_op jit(solution)/shard_map/band_forces/pallas_call | solution.py:691
  43.9 1.3 %write_out.1 = (bf16[64,15,8,128]{3,2,1,0:T(8,128)(2,1)}, f32[3,8,32]{2,1,0:T(8,128)}) custom-call(bf16[64,15,8,128]{3,2,1,0:T(8,128)(2,1)S(1)} %get-tuple-element.6.dens_in, f32[3,8,32]{2,1,0:T(8,128)S(1)} %get-tuple-element.7.force_in), custom_call_target="tpu_custom_call" | custom-call | tf_op jit(solution)/shard_map/write_out/pallas_call | solution.py:753
